TPU v7x, 128 devices: a whole 4x4x4 slice. The times are simulated.
128 devices in a mesh: dp: 1, tp: 16 (over z, y), cp: 8 (over x, core).
Axes of the slice: x: 4, y: 4, z: 4, core: 2. Of those that a mesh axis runs over, the one named last changes fastest.
Arguments:
- x: bfloat16 [4096, 8192], P(('dp', 'cp'))
- doc_ids: int32 [4096], P(('dp', 'cp'))
- w_query: bfloat16 [8192, 8192], P(None, 'tp')
- w_key: bfloat16 [8192, 8192], P(None, 'tp')
- w_value: bfloat16 [8192, 8192], P(None, 'tp')
- w_out: bfloat16 [8192, 8192], P('tp')
Outputs:
- output: bfloat16 [4096, 8192], P(('dp', 'cp'))
All inputs are finite; a program needn't handle non-finite values.
Results may differ from a plain program's by a relative error of at most 0.0071832.
Values are sent between devices in bfloat16 or wider.
A program may use at most 1 GiB of HBM per device.

v0:
```python
import jax
import jax.numpy as jnp
from jax import lax
from jax.experimental import pallas as pl
from jax.experimental.pallas import tpu as pltpu
from jax.sharding import PartitionSpec as P

MESH = pl.DeviceIdType.MESH
HD = 128
NX = 4
L = 512
D = 8192
F = 512
KC = 1024
NKC = D // KC
NB = 6
ROWS = ((0, 64), (64, 64), (128, 128), (256, 128), (384, 64), (448, 64))
R = len(ROWS)
Y_ORDER = (0, 1, 1, 0, 1, 1)
Y_DIR = ((1, 3), (1, 1), (3, 3), (1, 1), (3, 1), (3, 3))
O_FIRST = (1, 1, 0, 0, 1, 0)
O_DIR = (1, 1, 3, 1, 3, 3)
ORDER = (
    ("ostart", 5,), ("ostart", 1,), ("ostart", 0,), ("ofw0", 5,), ("ostart", 2,), ("opair", 5,),
    ("opair", 1,), ("opair", 0,), ("ofw1", 5,), ("wxl",), ("ofw0", 1,), ("opair", 2,),
    ("ofw1", 1,), ("ofw0", 0,), ("ostart", 4,), ("ofw0", 2,), ("mm0", 5,), ("ofw0", 4,),
    ("mm1", 5,), ("ofw1", 0,), ("mm0", 1,), ("mm1", 1,), ("ofw1", 2,), ("ostart", 3,),
    ("opair", 4,), ("yst", 5,), ("mm0", 0,), ("yst", 1,), ("ofw0", 3,), ("ofw1", 4,),
    ("mm0", 2,), ("opair", 3,), ("yf", 5, 0,), ("mm1", 0,), ("ym0", 5,), ("ym0", 1,),
    ("mm0", 4,), ("ym1", 5,), ("mm1", 2,), ("mm1", 4,), ("ym1", 1,), ("ofw1", 3,),
    ("yst", 2,), ("ym2", 5,), ("yst", 4,), ("ym2", 1,), ("mm0", 3,), ("mm1", 3,),
    ("yst", 0,), ("ym1", 2,), ("ym1", 4,), ("ym0", 0,), ("ym0", 4,), ("yst", 3,),
    ("yf", 5, 3,), ("ym2", 0,), ("ym1", 0,), ("yf", 1, 2,), ("ym0", 2,), ("ym1", 3,),
    ("ym0", 3,), ("yf", 2, 0,), ("yf", 4, 1,), ("ym2", 4,), ("yf", 5, 1,), ("yf", 0, 1,),
    ("yf", 3, 2,), ("yf", 5, 2,), ("ym2", 3,), ("yf", 2, 1,), ("yf", 1, 3,), ("yf", 0, 2,),
    ("ym2", 2,), ("yf", 3, 0,), ("yf", 1, 1,), ("yf", 1, 0,), ("yf", 0, 0,), ("yf", 4, 2,),
    ("yf", 3, 3,), ("yf", 4, 0,), ("yf", 2, 2,), ("yf", 3, 1,), ("yf", 4, 3,), ("yf", 2, 3,),
    ("yf", 0, 3,), ("ye", 4,), ("ye", 0,), ("ye", 2,), ("ye", 5,), ("ye", 1,),
    ("ye", 3,),
)
HL = L // 2
SCALE = (HD ** -0.5) * 1.4426950408889634
U = 16
DR = L - 8 * U
BF = jnp.bfloat16
F32 = jnp.float32


def mod(a, n):
    return lax.rem(a + n, n)


def kernel(x_hbm, seg_hbm, wq_hbm, wk_hbm, wv_hbm, wo_hbm, yg,
           xbuf, wbuf, acc, kloc, vloc, qloc, kg, vg, qg, obuf, og, wt, psend, pown, rsb, segs, sk, m_s, l_s, o_s,
           x_sem, w_sem, wo_sem, ws_send, ws_recv, wf_send, wf_recv, sh_send, sh_recv, wx_send, wx_recv,
           kv_send, kv_recv, kf_recv, q_send, q_recv, o_send, o_recv,
           sg_send, sg_recv, sg_loc, a_send, a_recv, r_send, r_recv, y_send, y_recv):
    t = lax.axis_index("tp")
    c = lax.axis_index("cp")
    x, k = c // 2, lax.rem(c, 2)
    z, y = t // NX, lax.rem(t, NX)
    yh, yb = y // 2, lax.rem(y, 2)
    xodd = lax.rem(x, 2)
    partner = {"cp": x * 2 + 1 - k}

    def iy(yy):
        return lax.rem(yy + yy // 2, 2)

    def slice_of(zz, yy):
        return zz * 2 + iy(yy)

    def piece_of(zz, yy):
        return slice_of(zz, yy) * 2 + yy // 2

    def tpdev(zz, yy):
        return {"tp": zz * NX + yy}

    def rcopy(src, dst, ss, rs, dev):
        return pltpu.make_async_remote_copy(src_ref=src, dst_ref=dst, send_sem=ss, recv_sem=rs, device_id=dev, device_id_type=MESH)

    s_me = z * 2 + yb
    sl_me = slice_of(z, y)
    sends = []

    def x_copy(i):
        return pltpu.make_async_copy(x_hbm.at[:, pl.ds(pl.multiple_of(i * KC, KC), KC)], xbuf.at[i], x_sem.at[i])

    w_hbms = (wk_hbm, wv_hbm, wq_hbm)

    def w_copies(w, i):
        g = lax.rem(4 * w + i, 3) * 2
        return [pltpu.make_async_copy(w_hbms[w].at[pl.ds(pl.multiple_of((2 * i + b) * KC, KC), KC), :], wbuf.at[g + b], w_sem.at[g + b]) for b in range(2)]

    def load(w, i):
        for b, cp_ in enumerate(w_copies(w, i)):
            if w == 0:
                x_copy(2 * i + b).start()
            cp_.start()

    for i in range(2):
        load(0, jnp.int32(i))
    seg_own = pltpu.make_async_copy(seg_hbm, segs.at[c], sg_loc)
    seg_own.start()
    my_cols = pl.ds(pl.multiple_of(sl_me * 1024, 1024), 1024)

    def share(cc):
        return pl.ds(pl.multiple_of(DR + cc * U, 8), U)

    wo_own = [pltpu.make_async_copy(wo_hbm.at[pl.ds(0, DR), my_cols], wt.at[s_me, pl.ds(0, DR), :], wo_sem.at[0]),
              pltpu.make_async_copy(wo_hbm.at[share(c), my_cols], wt.at[s_me, share(c), :], wo_sem.at[1])]

    bar = pltpu.get_barrier_semaphore()
    n_peers = 0
    for dc in range(1, 2 * NX):
        pl.semaphore_signal(bar, inc=1, device_id={"cp": mod(c + dc, 2 * NX)}, device_id_type=MESH)
        n_peers += 1
    for dz in range(NX):
        for e in range(2):
            if dz or e:
                pl.semaphore_signal(bar, inc=1, device_id=tpdev(mod(z + dz, NX), yh * 2 + lax.rem(yb + e, 2)), device_id_type=MESH)
                n_peers += 1
    pl.semaphore_signal(bar, inc=1, device_id=tpdev(z, 3 - y), device_id_type=MESH)
    n_peers += 1

    HR = DR // 2

    def w_move(dz, e, shared):
        z2, y2 = mod(z + dz, NX), yh * 2 + lax.rem(yb + e, 2)
        i = dz * 2 + e - 1
        rows = share(c) if shared else pl.ds(pl.multiple_of(k * HR, HR), HR)
        return rcopy(wo_hbm.at[rows, pl.ds(pl.multiple_of(slice_of(z2, y2) * 1024, 1024), 1024)], wt.at[s_me, rows, :],
                     sh_send if shared else ws_send, sh_recv.at[i] if shared else ws_recv.at[i], tpdev(z2, y2))

    def w_slot(dz, e):
        return mod(z - dz, NX) * 2 + lax.rem(yb + e, 2)

    def w_rows(dz, e, kk):
        return wt.at[w_slot(dz, e), pl.ds(pl.multiple_of(kk * HR, HR), HR), :]

    def w_fwd(dz, e, kk):
        i = dz * 2 + e - 1
        ref = w_rows(dz, e, kk)
        return rcopy(ref, ref, wf_send, wf_recv.at[i], partner)

    def wx(idx, cc, half, dev):
        cols = pl.ds(0, 1024) if half is None else pl.ds(half * 512, 512)
        ref = wt.at[:, share(cc), cols]
        return rcopy(ref, ref, wx_send, wx_recv.at[idx], dev)

    def xdev(dx):
        return {"cp": mod(x + dx, NX) * 2 + k}

    def blk(dx, kk):
        return mod(x + dx, NX) * 2 + kk

    def go(cp_):
        cp_.start()

    def wx_start():
        for dz, e in group:
            i = dz * 2 + e - 1
            ref = wt.at[w_slot(dz, e), share(c), :]
            rcopy(ref, ref, sh_send, sh_recv.at[i], partner).wait_recv()
        wo_own[1].wait()
        go(wx(0, c, 0, xdev(1)))
        go(wx(1, c, 1, xdev(3)))
        go(wx(2, c, None, partner))

    def wx_second():
        go(wx(8, c, 1, xdev(1)))
        go(wx(9, c, 0, xdev(3)))

    def wx_relay():
        wx(0, blk(3, k), 0, partner).wait_recv()
        go(wx(3, blk(3, k), 0, xdev(1)))
        wx(1, blk(1, k), 1, partner).wait_recv()
        go(wx(5, blk(1, k), 1, xdev(3)))

    def wx_last():
        w_forward((2,))
        wx(8, blk(3, k), 1, partner).wait_recv()
        go(wx(4, blk(3, k), None, partner))
        wx(9, blk(1, k), 0, partner).wait_recv()
        go(wx(6, blk(1, k), None, partner))
        wx(3, blk(2, k), 0, partner).wait_recv()
        wx(5, blk(2, k), 1, partner).wait_recv()
        go(wx(7, blk(2, k), None, partner))

    def w_forward(dzs):
        for dz, e in [g for g in group if g[0] in dzs]:
            i = dz * 2 + e - 1
            ref = w_rows(dz, e, k)
            rcopy(ref, ref, ws_send, ws_recv.at[i], partner).wait_recv()
            go(w_fwd(dz, e, k))

    def w_done():
        wo_own[0].wait()
        for dz, e in group:
            w_fwd(dz, e, 1 - k).wait_recv()
        wx(2, blk(0, 1 - k), None, partner).wait_recv()
        wx(4, blk(3, 1 - k), None, partner).wait_recv()
        wx(6, blk(1, 1 - k), None, partner).wait_recv()
        wx(7, blk(2, 1 - k), None, partner).wait_recv()

    group = [(dz, e) for dz in range(NX) for e in range(2) if dz or e]
    def spread_w():
        pl.semaphore_wait(bar, n_peers)
        seg_own.wait()
        for dc in range(1, 2 * NX):
            cp_ = rcopy(segs.at[c], segs.at[c], sg_send, sg_recv.at[dc - 1], {"cp": mod(c + dc, 2 * NX)})
            cp_.start()
        for shared in (True, False):
            for dz, e in group:
                go(w_move(dz, e, shared))
        for cp_ in reversed(wo_own):
            cp_.start()

    def project(w, lo, hi):
        def step(i, _):
            nxt = i + 2

            @pl.when(nxt < NKC // 2)
            def _():
                load(w, nxt)
            if w < 2:
                @pl.when(nxt >= NKC // 2)
                def _():
                    load(w + 1, nxt - NKC // 2)
            for b, cp_ in enumerate(w_copies(w, i)):
                cp_.wait()
                if w == 0:
                    x_copy(2 * i + b).wait()
            g = lax.rem(4 * w + i, 3) * 2
            acc[...] += (jnp.dot(xbuf[2 * i], wbuf[g], preferred_element_type=F32)
                         + jnp.dot(xbuf[2 * i + 1], wbuf[g + 1], preferred_element_type=F32))
            return 0
        lax.fori_loop(lo, hi, step, 0)

    def split(dst):
        for h in range(4):
            dst[h] = acc[:, h * HD:(h + 1) * HD].astype(BF)

    def kv_copy(n, idx, src, dst, dev):
        return rcopy(src, dst, kv_send.at[n], kv_recv.at[n, idx], dev)

    def kv_spread(n, loc, gat):
        for dx in (2, 1, 3):
            go(kv_copy(n, dx - 1, loc.at[mod(x + dx, NX)], gat.at[c], xdev(dx)))
        go(kv_copy(n, 3, loc.at[x], gat.at[c], partner))
        gat[c] = loc[x]

    def kv_forward(n, gat):
        for dx in (1, 3, 2):
            ref = gat.at[blk(4 - dx, k)]
            kv_copy(n, dx - 1, ref, ref, partner).wait_recv()
            go(rcopy(ref, ref, kv_send.at[n], kf_recv.at[n, dx - 1], partner))

    def kv_partner(n, gat):
        ref = gat.at[blk(0, 1 - k)]
        kv_copy(n, 3, ref, ref, partner).wait_recv()

    def kv_finish(n, gat):
        for dx in (1, 3, 2):
            ref = gat.at[blk(4 - dx, 1 - k)]
            rcopy(ref, ref, kv_send.at[n], kf_recv.at[n, dx - 1], partner).wait_recv()

    acc[...] = jnp.zeros_like(acc)
    with jax.named_scope("proj_k0"):
        project(0, 0, 2)
    with jax.named_scope("barrier"):
        spread_w()
    with jax.named_scope("proj_k1"):
        project(0, 2, 4)
    split(kloc)
    acc[...] = jnp.zeros_like(acc)
    kv_spread(0, kloc, kg)
    with jax.named_scope("proj_v"):
        project(1, 0, 4)
    for h in range(4):
        vloc[h] = jnp.transpose(acc[:, h * HD:(h + 1) * HD]).astype(BF)
    acc[...] = jnp.zeros_like(acc)
    kv_spread(1, vloc, vg)
    with jax.named_scope("proj_q0"):
        project(2, 0, 2)
    with jax.named_scope("fwd_k"):
        kv_forward(0, kg)
    with jax.named_scope("proj_q1"):
        project(2, 2, 4)
    split(qloc)
    own = lax.rem(x + k, 2)
    for dx in (2, 1, 3):
        h = mod(x + dx, NX)
        cp_ = rcopy(qloc.at[h], qg.at[x], q_send.at[dx - 1], q_recv.at[x], {"cp": h * 2 + own})
        cp_.start()
        sends.append(cp_)

    @pl.when(xodd == 0)
    def _():
        qg[x] = qloc[x]

    q_d2d = rcopy(qloc.at[x], qg.at[x], q_send.at[3], q_recv.at[x], partner)

    @pl.when(xodd == 1)
    def _():
        q_d2d.start()

    with jax.named_scope("segs"):
        for dc in range(1, 2 * NX):
            ref = segs.at[mod(c - dc, 2 * NX)]
            rcopy(ref, ref, sg_send, sg_recv.at[dc - 1], partner).wait_recv()

        def seg_columns(j, _):
            sk[j] = jnp.transpose(jnp.broadcast_to(segs[j], (HD, L)))
            return 0
        lax.fori_loop(0, 2 * NX, seg_columns, 0)
    tiles = [slice(b, b + HL) for b in range(0, L, HL)]

    def q_block(xx):
        return 2 * xx + lax.rem(k + xx, 2)

    def local(xx):
        return (x == xx) & (xodd == 0)

    def scores(xx, j, n, rows, diag):
        s = lax.dot_general(kg[j, 0:n, :], qg[xx, rows, :], (((1,), (1,)), ((), ())), preferred_element_type=F32)
        ok = jnp.concatenate([sk[j, 0:n, :]] * (HL // HD), axis=1) == jnp.broadcast_to(segs[q_block(xx)][:, rows], (n, HL))
        if diag:
            qi = lax.broadcasted_iota(jnp.int32, (n, HL), 1) + rows.start
            ok = ok & (lax.broadcasted_iota(jnp.int32, (n, HL), 0) <= qi)
        return jnp.where(ok, s * SCALE, -jnp.inf)

    def update(xx, blocks):
        for rows in tiles:
            ss = [scores(xx, j, L, rows, False) for j in blocks]
            m = m_s[xx, :, rows]
            m_new = m
            for s in ss:
                m_new = jnp.maximum(m_new, jnp.max(s, axis=0, keepdims=True))
            alpha = jnp.exp2(m - m_new)
            l, o = l_s[xx, :, rows] * alpha, o_s[xx, :, rows] * alpha
            for j, s in zip(blocks, ss):
                p = jnp.exp2(s - m_new)
                l += jnp.sum(p, axis=0, keepdims=True)
                o += jnp.dot(vg[j], p.astype(BF), preferred_element_type=F32)
            m_s[xx, :, rows], l_s[xx, :, rows], o_s[xx, :, rows] = m_new, l, o

    def o_ret(xx):
        ocol = pl.ds(pl.multiple_of(s_me * F + x * HD, HD), HD)
        return rcopy(obuf.at[xx], og.at[:, ocol], o_send.at[xx], o_recv.at[x], {"cp": q_block(xx)}), ocol

    def finish(xx):
        obuf[xx] = jnp.transpose(o_s[xx] / l_s[xx]).astype(BF)
        ret, ocol = o_ret(xx)

        @pl.when(local(xx))
        def _():
            og[:, ocol] = obuf[xx]

        pl.when(jnp.logical_not(local(xx)))(ret.start)

    def q_in(a):
        xx = mod(x + a, NX)
        return rcopy(qg.at[xx], qg.at[xx], q_send.at[3], q_recv.at[xx], partner)

    def attend_own(a):
        xx = mod(x + a, NX)
        c_q = q_block(xx)
        for rows in tiles:
            s = scores(xx, c_q, rows.stop, rows, True)
            m = jnp.max(s, axis=0, keepdims=True)
            p = jnp.exp2(s - m)
            m_s[xx, :, rows] = m
            l_s[xx, :, rows] = jnp.sum(p, axis=0, keepdims=True)
            o_s[xx, :, rows] = jnp.dot(vg[c_q, :, 0:rows.stop], p.astype(BF), preferred_element_type=F32)

    def attend_before(xx):
        def chip_step(i, _):
            update(xx, [2 * i, 2 * i + 1])
            return 0
        lax.fori_loop(0, xx, chip_step, 0)
        finish(xx)

    def wait_o():
        for h in range(NX):
            o_in = rcopy(obuf.at[0], og.at[:, pl.ds(pl.multiple_of(s_me * F + h * HD, HD), HD)], o_send.at[0], o_recv.at[h], partner)
            pl.when(jnp.logical_not((x == h) & (xodd == 0)))(o_in.wait_recv)

    with jax.named_scope("own0"):
        kv_partner(0, kg)
        kv_partner(1, vg)
        pl.when(xodd == 1)(q_in(0).wait_recv)
        attend_own(0)
    with jax.named_scope("fwd_v"):
        kv_forward(1, vg)

    with jax.named_scope("fin_kv"):
        kv_finish(0, kg)
        kv_finish(1, vg)
    with jax.named_scope("own1"):
        q_in(1).wait_recv()
        q_in(3).wait_recv()
        wx_start()
        attend_own(1)
        attend_own(3)
        wx_second()
    with jax.named_scope("own2"):
        q_in(2).wait_recv()
        attend_own(2)
        for xx in (1 - k, 3 - k):
            update(xx, [2 * xx])
    for a in (2, 3, 1, 0):
        with jax.named_scope("attn%d" % a):
            attend_before(mod(x + a, NX))
    def row_ds(r):
        return pl.ds(ROWS[r][0], ROWS[r][1])

    def o_copy(r, idx, zz, e, dev):
        s = zz * 2 + lax.rem(yb + e, 2)
        ref = og.at[row_ds(r), pl.ds(pl.multiple_of(s * F, F), F)]
        return rcopy(ref, ref, a_send, a_recv.at[r, idx], dev)

    def o_send_z(r, e):
        d = O_DIR[r]
        go(o_copy(r, 1 + 3 * e, z, e, tpdev(mod(z + d, NX), y)))
        go(o_copy(r, 2 + 3 * e, z, e, tpdev(mod(z + NX - d, NX), y)))

    pair = tpdev(z, yh * 2 + 1 - yb)
    o_seen = []

    def ostart(r):
        if not o_seen:
            o_seen.append(r)
            with jax.named_scope("wait_o"):
                wait_o()
        go(o_copy(r, 0, z, 0, pair))
        o_send_z(r, 0)
        if len(o_seen) == 1:
            o_seen.append(r)
            wx_relay()
            w_forward((0, 1, 3))

    def o_forward(r, e):
        d = O_DIR[r]
        zz = mod(z + NX - d, NX)
        o_copy(r, 1 + 3 * e, zz, e, partner).wait_recv()
        go(o_copy(r, 3 + 3 * e, zz, e, tpdev(mod(z + d, NX), y)))

    def o_pair(r, idx, new, zz):
        o_copy(r, idx, zz, 0, partner).wait_recv()
        go(o_copy(r, new, zz, 0, pair))

    def opair(r):
        if O_FIRST[r] == 0:
            o_pair(r, 2, 5, mod(z + O_DIR[r], NX))
            return
        o_copy(r, 0, z, 1, partner).wait_recv()
        o_send_z(r, 1)

    def ofw0(r):
        o_forward(r, 0)
        if O_FIRST[r] == 0:
            go(o_copy(r, 4, mod(z + NX - O_DIR[r], NX), 0, pair))

    def ofw1(r):
        if O_FIRST[r] == 0:
            o_pair(r, 3, 6, mod(z + 2, NX))
            return
        o_forward(r, 1)

    def o_rest(r):
        d = O_DIR[r]
        if O_FIRST[r] == 0:
            for idx, zz in ((0, z), (4, mod(z + NX - d, NX)), (5, mod(z + d, NX)), (6, mod(z + 2, NX))):
                o_copy(r, idx, zz, 1, partner).wait_recv()
            return
        for e in range(2):
            o_copy(r, 2 + 3 * e, mod(z + d, NX), e, partner).wait_recv()
            o_copy(r, 3 + 3 * e, mod(z + 2, NX), e, partner).wait_recv()

    def matmul(r, half):
        out = psend if half == 0 else pown
        hh = (1 - yh) if half == 0 else yh
        a, n = ROWS[r]
        for b in range(2):
            cols = pl.ds(pl.multiple_of(hh * F + b * 256, 256), 256)
            out[a:a + n, b * 256:(b + 1) * 256] = jnp.dot(og[a:a + n, :], wt[:, :, cols].reshape(8 * F, 256), preferred_element_type=F32)

    def rs_copy(r):
        return rcopy(psend.at[row_ds(r), :], rsb.at[row_ds(r), :], r_send, r_recv.at[r], tpdev(z, 3 - y))

    def mm0(r):
        o_rest(r)
        if r == first_mm:
            with jax.named_scope("w_done"):
                w_done()
        matmul(r, 0)
        go(rs_copy(r))

    def y_pos(r, a, b):
        if Y_ORDER[r] == 0:
            return mod(z + a, NX), mod(y + b, NX)
        return mod(z + b, NX), mod(y + a, NX)

    def y_ref(r, pos):
        return yg.at[row_ds(r), pl.ds(pl.multiple_of(piece_of(*pos) * F, F), F)]

    def y_copy(r, idx, pos, dev):
        ref = y_ref(r, pos)
        return rcopy(ref, ref, y_send, y_recv.at[r, idx], dev)

    def y_second(r, j, a):
        d2 = Y_DIR[r][1]
        pos = y_pos(r, a, 0)
        go(y_copy(r, 3 + 3 * j, pos, tpdev(*y_pos(r, 0, d2))))
        go(y_copy(r, 4 + 3 * j, pos, tpdev(*y_pos(r, 0, NX - d2))))

    def yst(r):
        rs_copy(r).wait_recv()
        a, n = ROWS[r]
        yg[a:a + n, pl.ds(pl.multiple_of(piece_of(z, y) * F, F), F)] = (pown[a:a + n, :] + rsb[a:a + n, :]).astype(BF)
        d = Y_DIR[r][0]
        pos = y_pos(r, 0, 0)
        go(y_copy(r, 0, pos, tpdev(*y_pos(r, d, 0))))
        go(y_copy(r, 1, pos, tpdev(*y_pos(r, NX - d, 0))))
        y_second(r, 0, 0)

    def ym0(r):
        d = Y_DIR[r][0]
        pos = y_pos(r, NX - d, 0)
        y_copy(r, 0, pos, partner).wait_recv()
        go(y_copy(r, 2, pos, tpdev(*y_pos(r, d, 0))))
        y_second(r, 1, NX - d)

    def ym1(r):
        d = Y_DIR[r][0]
        y_copy(r, 1, y_pos(r, d, 0), partner).wait_recv()
        y_second(r, 2, d)

    def ym2(r):
        y_copy(r, 2, y_pos(r, 2, 0), partner).wait_recv()
        y_second(r, 3, 2)

    def y_offs(r):
        d = Y_DIR[r][0]
        return (0, NX - d, d, 2)

    def yf(r, j):
        d2 = Y_DIR[r][1]
        pos = y_pos(r, y_offs(r)[j], NX - d2)
        y_copy(r, 3 + 3 * j, pos, partner).wait_recv()
        go(y_copy(r, 5 + 3 * j, pos, tpdev(*y_pos(r, 0, d2))))

    def ye(r):
        d2 = Y_DIR[r][1]
        for j, a in enumerate(y_offs(r)):
            y_copy(r, 4 + 3 * j, y_pos(r, a, d2), partner).wait_recv()
            y_copy(r, 5 + 3 * j, y_pos(r, a, 2), partner).wait_recv()

    steps = dict(ostart=ostart, opair=opair, ofw0=ofw0, ofw1=ofw1, mm0=mm0,
                 mm1=lambda r: matmul(r, 1), wxl=wx_last, yst=yst, ym0=ym0, ym1=ym1, ym2=ym2, yf=yf, ye=ye)
    first_mm = [a[1] for a in ORDER if a[0] == "mm0"][0]
    def drain(ref, sem):
        rcopy(ref, ref, sem, r_recv.at[0], partner).wait_send()

    def drain_early():
        drain(segs.at[pl.ds(0, 7)], sg_send)
        drain(kg.at[pl.ds(0, 7)], kv_send.at[0])
        drain(vg.at[pl.ds(0, 7)], kv_send.at[1])
        drain(wt.at[pl.ds(0, 7), pl.ds(0, HR), :], ws_send)
        drain(wt.at[pl.ds(0, 7), pl.ds(0, U), :], sh_send)
        drain(wt.at[pl.ds(0, 7), pl.ds(0, HR), :], wf_send)
        drain(wt.at[:, pl.ds(0, 7 * U), :], wx_send)
        for cp_ in sends:
            cp_.wait_send()

        @pl.when(xodd == 1)
        def _():
            q_d2d.wait_send()

        for xx in range(NX):
            pl.when(jnp.logical_not(local(xx)))(o_ret(xx)[0].wait_send)

    last_y = [a[1] for a in ORDER if a[0] == "yst"][-1]
    for name, *args in ORDER:
        with jax.named_scope(name + "_".join(str(a) for a in args)):
            steps[name](*args)
        if name == "yst" and args[0] == last_y:
            drain_early()

    drain(psend, r_send)
    drain(og.at[:, pl.ds(0, 7 * F)], a_send)
    drain(yg.at[:, pl.ds(0, 15 * F)], y_send)


def solution(mesh):
    def body(x, doc, wq, wk, wv, wo):
        seg = doc.reshape(1, L)
        dma = pltpu.SemaphoreType.DMA
        any_ = pl.BlockSpec(memory_space=pl.ANY)
        return pl.pallas_call(
            kernel,
            out_shape=pltpu.VMEM((L, D), BF),
            in_specs=[any_] * 6,
            out_specs=pl.BlockSpec(memory_space=pltpu.VMEM),
            scratch_shapes=[
                pltpu.VMEM((NKC, L, KC), BF), pltpu.VMEM((NB, KC, F), BF), pltpu.VMEM((L, F), F32),
                pltpu.VMEM((4, L, HD), BF), pltpu.VMEM((4, HD, L), BF), pltpu.VMEM((4, L, HD), BF),
                pltpu.VMEM((8, L, HD), BF), pltpu.VMEM((8, HD, L), BF), pltpu.VMEM((4, L, HD), BF), pltpu.VMEM((4, L, HD), BF),
                pltpu.VMEM((L, 8 * F), BF), pltpu.VMEM((8, F, 1024), BF),
                pltpu.VMEM((L, F), F32), pltpu.VMEM((L, F), F32), pltpu.VMEM((L, F), F32),
                pltpu.VMEM((8, 1, L), jnp.int32), pltpu.VMEM((8, L, HD), jnp.int32),
                pltpu.VMEM((NX, 1, L), F32), pltpu.VMEM((NX, 1, L), F32), pltpu.VMEM((NX, HD, L), F32),
                dma((NKC,)), dma((NB,)), dma((2,)), dma, dma((7,)), dma, dma((7,)), dma, dma((7,)), dma, dma((10,)),
                dma((2,)), dma((2, 4)), dma((2, 3)), dma((4,)), dma((4,)), dma((4,)), dma((4,)),
                dma, dma((7,)), dma, dma, dma((R, 7)), dma, dma((R,)), dma, dma((R, 15)),
            ],
            compiler_params=pltpu.CompilerParams(collective_id=0, has_side_effects=True, vmem_limit_bytes=50 * 1024 * 1024),
        )(x, seg, wq, wk, wv, wo)

    return jax.shard_map(body, mesh=mesh, in_specs=(P(('dp', 'cp'), None), P(('dp', 'cp')), P(None, 'tp'), P(None, 'tp'), P(None, 'tp'), P('tp', None)), out_specs=P(('dp', 'cp'), None), check_vma=False)
```

profile of v0, /device:TPU:2, one launch (start us, length us, event | category | flops | bytes accessed | tf_op | source)
XLA Modules:
  0.0 127.2 jit_solution(12469989411149570600)
XLA Ops:
  0.0 123.8 %shard_map.64 = bf16[512,8192]{1,0:T(8,128)(2,1)S(1)} custom-call(bf16[512,8192]{1,0:T(8,128)(2,1)} %x_hbm.1, s32[1,512]{1,0:T(1,128)} %bitcast.1, bf16[8192,512]{1,0:T(8,128)(2,1)} %wq_hbm.1, bf16[8192,512]{1,0:T(8,128)(2,1)} %wk_hbm.1, bf16[8192,512]{1,0:T(8,128)(2,1)} %wv_hbm.1, bf16[512,8192]{1,0:T(8,128)(2,1)} %wo_hbm.1), custom_call_target="tpu_custom_call" | custom-call | tf_op jit(solution)/shard_map/pallas_call | solution.py:600
  123.8 3.4 %copy.8 = bf16[512,8192]{1,0:T(8,128)(2,1)} copy(bf16[512,8192]{1,0:T(8,128)(2,1)S(1)} %shard_map.64) | data formatting | bytes 16777216
where the time goes:
time: 127 us
  Pallas kernels  124 us (98%)
  local copies, waits for them, and re-layouts  3.4 us (3%)
    pallas_call x1, Pallas kernels, body(): pl.pallas_call(kernel, out_shape=pltpu.VMEM((L, D), BF), in_specs=[any_]...  124 us
    unnamed x1, local copies, waits for them, and re-layouts  3.4 us

commit v1 on v0

--- a/solution.py
+++ b/solution.py
@@ -210,7 +210,7 @@
             cp_ = rcopy(segs.at[c], segs.at[c], sg_send, sg_recv.at[dc - 1], {"cp": mod(c + dc, 2 * NX)})
             cp_.start()
         for shared in (True, False):
-            for dz, e in group:
+            for dz, e in sorted(group, key=lambda g: g[0] != 2):
                 go(w_move(dz, e, shared))
         for cp_ in reversed(wo_own):
             cp_.start()

time: 127 us -> 128 us (level)
  no operation moved by 1% of the time
where the time goes in v1:
time: 128 us
  Pallas kernels  124 us (97%)
  local copies, waits for them, and re-layouts  3.4 us (3%)
    pallas_call x1, Pallas kernels, body(): pl.pallas_call(kernel, out_shape=pltpu.VMEM((L, D), BF), in_specs=[any_]...  124 us
    unnamed x1, local copies, waits for them, and re-layouts  3.4 us

profile of v1, /device:TPU:2, one launch (start us, length us, event | category | flops | bytes accessed | tf_op | source)
XLA Modules:
  0.0 127.6 jit_solution(17463802769831560028)
XLA Ops:
  0.0 124.2 %shard_map.64 = bf16[512,8192]{1,0:T(8,128)(2,1)S(1)} custom-call(bf16[512,8192]{1,0:T(8,128)(2,1)} %x_hbm.1, s32[1,512]{1,0:T(1,128)} %bitcast.1, bf16[8192,512]{1,0:T(8,128)(2,1)} %wq_hbm.1, bf16[8192,512]{1,0:T(8,128)(2,1)} %wk_hbm.1, bf16[8192,512]{1,0:T(8,128)(2,1)} %wv_hbm.1, bf16[512,8192]{1,0:T(8,128)(2,1)} %wo_hbm.1), custom_call_target="tpu_custom_call" | custom-call | tf_op jit(solution)/shard_map/pallas_call | solution.py:600
  124.2 3.4 %copy.8 = bf16[512,8192]{1,0:T(8,128)(2,1)} copy(bf16[512,8192]{1,0:T(8,128)(2,1)S(1)} %shard_map.64) | data formatting | bytes 16777216
